TPU v7x, 128 devices: a whole 4x4x4 slice. The times are simulated.
128 devices in a mesh: slab: 16 (over y, x), lev: 8 (over z, core).
Axes of the slice: x: 4, y: 4, z: 4, core: 2. Of those that a mesh axis runs over, the one named last changes fastest.
Arguments:
- ensemble: float32 [80, 32, 36864], P(None, 'lev', 'slab'), may hold values from -6 to 6
- obs_cell: int32 [2, 256], replicated, may hold values from 0 to 1179647, as said below
- obs_value: float32 [2, 256], replicated, may hold values from -6 to 6
- obs_var: float32 [2, 256], replicated, may hold values from 0.3 to 3
- obs_frac: float32 [2, 256], replicated, may hold values from 0 to 1
- loc_column: bfloat16 [2, 256, 36864], P(None, 'lev', 'slab'), may hold values from 0 to 1
- loc_level: float32 [2, 256, 32], P(None, None, 'lev'), may hold values from 0.2 to 1
Outputs:
- analysis: float32 [80, 32, 36864], P(None, 'lev', 'slab')
- prior_mean: float32 [2, 256], replicated
Inputs may be any that keep to these rules, and one draw needn't show every extreme that they name: `obs_cell`: in each block, every device's cells (a level band of 4 levels and a slab of 2304 columns) hold at least one observation, and one of them lies in the slab's last column.
All inputs are finite; a program needn't handle non-finite values.
Results may differ from a plain program's by a relative error of at most 0.0055.
Values may be sent and summed in bfloat16 or wider, within the bound.
A program may use at most 64 MiB of HBM per device.

v0:
```python
import jax
import jax.numpy as jnp
from jax import lax
from jax.sharding import PartitionSpec as P


def laid_out(parts, dim):
    parts = jnp.moveaxis(parts, 0, dim)
    shape = parts.shape
    return parts.reshape(*shape[:dim], shape[dim] * shape[dim + 1], *shape[dim + 2 :])


def sent_to_all(array, axis):
    copies = jnp.broadcast_to(array, (lax.axis_size(axis), *array.shape))
    return lax.all_to_all(copies, axis, split_axis=0, concat_axis=0, tiled=True)


def gather_directly(array, axis, dim):
    return laid_out(sent_to_all(array, axis), dim)


def obs_stats(prior_obs, obs_val, variance):
    members = prior_obs.shape[1]
    obs_mean = jnp.mean(prior_obs, axis=1)
    deviation = prior_obs - obs_mean[:, None]
    spread = jnp.sum(deviation * deviation, axis=1) / (members - 1.0)
    total_var = spread + variance
    shrink = 1.0 / (1.0 + jnp.sqrt(variance / total_var))
    gain_rows = ((obs_val - obs_mean)[:, None] - deviation * shrink[:, None]) / (
        total_var * (members - 1.0)
    )[:, None]
    return (obs_mean, deviation.astype(jnp.bfloat16), gain_rows.astype(jnp.bfloat16))


def cell_values(current, levels, columns):
    members, lev_rows, slab_cols = current.shape
    local_row = levels - lax.axis_index("lev") * lev_rows
    local_col = columns - lax.axis_index("slab") * slab_cols
    inside = (local_row >= 0) & (local_row < lev_rows) & (local_col >= 0) & (local_col < slab_cols)
    row_safe = jnp.clip(local_row, 0, lev_rows - 1)
    col_safe = jnp.clip(local_col, 0, slab_cols - 1)
    flattened = current.reshape(members, lev_rows * slab_cols)
    picked = jnp.take(flattened, row_safe * slab_cols + col_safe, axis=1)
    return jnp.where(inside[None, :], picked, 0.0).T


def column_table(loc_block, columns):
    rows_local, slab_cols = loc_block.shape
    local_col = columns - lax.axis_index("slab") * slab_cols
    inside = (local_col >= 0) & (local_col < slab_cols)
    col_safe = jnp.clip(local_col, 0, slab_cols - 1)
    picked = jnp.take(loc_block, col_safe, axis=1).astype(jnp.float32)
    picked = jnp.where(inside[None, :], picked, 0.0)
    holder = jnp.zeros((rows_local * lax.axis_size("lev"), columns.shape[0]), jnp.float32)
    return lax.dynamic_update_slice(
        holder, picked, (lax.axis_index("lev") * rows_local, jnp.int32(0))
    )


def level_table(lev_block, levels):
    lev_rows = lev_block.shape[1]
    local_row = levels - lax.axis_index("lev") * lev_rows
    inside = (local_row >= 0) & (local_row < lev_rows) & (lax.axis_index("slab") == 0)
    row_safe = jnp.clip(local_row, 0, lev_rows - 1)
    picked = jnp.take(lev_block, row_safe, axis=1)
    return jnp.where(inside[None, :], picked, 0.0)


def cell_update(values, dev_b, gain_b, col_table, lev_table):
    centred_cells = (values - jnp.mean(values, axis=1)[:, None]).astype(jnp.bfloat16)
    cross_cov = jnp.dot(dev_b, centred_cells.T, preferred_element_type=jnp.float32)
    mixed_rows = (lev_table * col_table * cross_cov).astype(jnp.bfloat16)
    return values + jnp.dot(gain_b.T, mixed_rows, preferred_element_type=jnp.float32).T


def regress_rows(running, loc_piece, row_start, centred, dev_b, gain_b, lev_weights):
    row_total = loc_piece.shape[0]
    row_step = min(row_total, 64)
    lev_rows = lev_weights.shape[1]
    slab_cols = loc_piece.shape[1]
    for offset in range(0, row_total, row_step):
        row_count = min(row_step, row_total - offset)
        row_piece = loc_piece[offset : offset + row_count]
        dev_rows = lax.dynamic_slice_in_dim(dev_b, row_start + offset, row_count, 0)
        gain_rows = lax.dynamic_slice_in_dim(gain_b, row_start + offset, row_count, 0)
        level_loc = lax.dynamic_slice_in_dim(lev_weights, row_start + offset, row_count, 0)
        cross_cov = jnp.dot(dev_rows, centred, preferred_element_type=jnp.float32).reshape(
            row_count, lev_rows, slab_cols
        )
        weights = level_loc[:, :, None] * row_piece[:, None, :].astype(jnp.float32)
        mixed_rows = (
            (weights * cross_cov).astype(jnp.bfloat16).reshape(row_count, lev_rows * slab_cols)
        )
        running = running + jnp.dot(gain_rows.T, mixed_rows, preferred_element_type=jnp.float32)
    return running


def on_device(ensemble, obs_cell, obs_value, obs_var, obs_frac, loc_column, loc_level):
    members, lev_rows, slab_cols = ensemble.shape
    n_blocks = obs_cell.shape[0]
    total_cols = slab_cols * lax.axis_size("slab")
    pair_index = {}
    pieces = []
    for later in range(n_blocks):
        levels = obs_cell[later] // total_cols
        columns = obs_cell[later] % total_cols
        next_cols = (columns + 1) % total_cols
        pieces.append(cell_values(ensemble, levels, columns))
        pieces.append(cell_values(ensemble, levels, next_cols))
        for earlier in range(later):
            pair_index[earlier, later] = len(pieces)
            pieces.append(column_table(loc_column[earlier], columns))
            pieces.append(column_table(loc_column[earlier], next_cols))
            pieces.append(level_table(loc_level[earlier], levels))
    summed = lax.psum(tuple(pieces), ("slab", "lev"))
    raw_first = []
    raw_second = []
    position = 0
    for later in range(n_blocks):
        raw_first.append(summed[position])
        raw_second.append(summed[position + 1])
        position = position + 2 + 3 * later
    columns_all = gather_directly(loc_column, "lev", 1)
    current = ensemble
    prior_means = []
    for block_index in range(n_blocks):
        fraction = obs_frac[block_index]
        prior_obs = (1.0 - fraction)[:, None] * raw_first[block_index] + fraction[
            :, None
        ] * raw_second[block_index]
        obs_mean, dev_b, gain_b = obs_stats(prior_obs, obs_value[block_index], obs_var[block_index])
        prior_means.append(obs_mean)
        centred = (
            (current - jnp.mean(current, axis=0))
            .astype(jnp.bfloat16)
            .reshape(members, lev_rows * slab_cols)
        )
        lev_weights = loc_level[block_index]
        zero_incr = jnp.zeros((members, lev_rows * slab_cols), jnp.float32)
        increment = regress_rows(
            zero_incr, columns_all[block_index], 0, centred, dev_b, gain_b, lev_weights
        )
        for later in range(block_index + 1, n_blocks):
            start_at = pair_index[block_index, later]
            col_first = summed[start_at]
            col_second = summed[start_at + 1]
            lev_table = summed[start_at + 2]
            raw_first[later] = cell_update(raw_first[later], dev_b, gain_b, col_first, lev_table)
            raw_second[later] = cell_update(raw_second[later], dev_b, gain_b, col_second, lev_table)
        current = current + increment.reshape(members, lev_rows, slab_cols)
    return (current, jnp.stack(prior_means))


def solution(mesh):
    in_specs = (
        P(None, "lev", "slab"),
        P(),
        P(),
        P(),
        P(),
        P(None, "lev", "slab"),
        P(None, None, "lev"),
    )
    out_specs = (P(None, "lev", "slab"), P())
    return jax.shard_map(
        on_device, mesh=mesh, in_specs=in_specs, out_specs=out_specs, check_vma=False
    )
```

profile of v0, /device:TPU:1, one launch (start us, length us, event | category | flops | bytes accessed | tf_op | source)
XLA Modules:
  0.0 267.5 jit_solution(16684422704884585923)
XLA Ops:
  7.2 2.6 broadcast_in_dim.147
  9.8 7.1 %all-to-all-start = ((bf16[8,2,32,2304]{3,2,1,0:T(8,128)(2,1)}), bf16[8,2,32,2304]{3,2,1,0:T(8,128)(2,1)}, u32[]{:S(2)}, u32[]{:S(2)}) async-start(bf16[8,2,32,2304]{3,2,1,0:T(8,128)(2,1)} %broadcast_in_dim.147), calls=%async_computation | async-start | bytes 4718592 | tf_op jit(solution)/shard_map/all_to_all | solution.py:15
  17.6 3.5 %copy.35 = f32[80,4,2304]{0,2,1:T(8,128)} copy(f32[80,4,2304]{2,1,0:T(4,128)S(1)} %copy-done) | data formatting | bytes 5898240 | tf_op args[0]
  21.7 1.1 and_reduce_fusion.6
  23.4 3.7 %gather_fusion.2 = f32[256,80]{1,0:T(8,128)} fusion(f32[80,9216]{0,1:T(8,128)} %bitcast.212, s32[1024]{0:T(1024)S(1)} %pad_clamp_fusion.5), kind=kCustom, calls=%fused_computation.2.clone | custom fusion | bytes 164864 | tf_op jit(solution)/shard_map/jit(_take)/gather | solution.py:43
  27.1 3.7 %gather_fusion.1 = f32[256,80]{1,0:T(8,128)} fusion(f32[80,9216]{0,1:T(8,128)} %bitcast.213, s32[1024]{0:T(1024)S(1)} %pad_clamp_fusion.6), kind=kCustom, calls=%fused_computation.clone | custom fusion | bytes 164864 | tf_op jit(solution)/shard_map/jit(_take)/gather | solution.py:43
  32.5 3.7 %gather_fusion.3 = f32[256,80]{1,0:T(8,128)} fusion(f32[80,9216]{0,1:T(8,128)} %bitcast.214, s32[1024]{0:T(1024)S(1)} %pad_clamp_fusion.4), kind=kCustom, calls=%fused_computation.3.clone | custom fusion | bytes 164864 | tf_op jit(solution)/shard_map/jit(_take)/gather | solution.py:43
  38.0 1.2 copy.61
  39.3 1.5 gather_fusion.4
  41.6 1.3 pad_clamp_fusion.1
  42.9 3.8 %gather_fusion.5 = f32[256,80]{1,0:T(8,128)} fusion(f32[80,9216]{0,1:T(8,128)} %bitcast.215, s32[1024]{0:T(1024)} %pad_clamp_fusion.1), kind=kCustom, calls=%fused_computation.4.clone | custom fusion | bytes 164864 | tf_op jit(solution)/shard_map/jit(_take)/gather | solution.py:43
  46.7 1.2 pad_clamp_fusion
  48.0 1.6 gather_fusion.6
  50.5 1.7 fusion.45
  52.2 1.7 fusion.46
  54.7 1.7 fusion.44
  56.4 1.7 select_bitcast_fusion
  58.1 1.5 fusion.43
  61.7 1.7 subtract_convert_fusion.1
  63.4 150.0 %all-reduce.3.cloned.1.call-done = (f32[256,80]{1,0:T(8,128)}, f32[256,80]{1,0:T(8,128)}, f32[256,80]{1,0:T(8,128)}, f32[256,256]{1,0:T(8,128)}, f32[256,256]{1,...) async-done(((f32[256,80]{1,0:T(8,128)}, f32[256,80]{1,0:T(8,128)}, f32[256,80]{1,0:T(8,128)}, f32[256,256]{1,0:T(8,128)}, f32[256,256]{1,0:T(8,128)}, ...) | async-done | bytes 1114128 | tf_op jit(solution)/shard_map/psum | solution.py:115
  213.3 1.0 reduce_sum.75
  214.4 1.2 fusion.80
  217.1 2.3 fusion.32
  219.4 1.7 fusion.87
  222.8 2.6 fusion.83
  225.5 1.2 copy-done.1
  233.2 2.2 convolution_add_fusion.3
  235.4 4.5 %reshape.387 = f32[80,4,2304]{2,1,0:T(4,128)} reshape(f32[80,9216]{1,0:T(8,128)} %convolution_add_fusion.3) | data formatting | bytes 5898240 | tf_op jit(solution)/shard_map/reshape | solution.py:150
  239.9 2.8 %fusion.79 = (f32[4,2304]{1,0:T(4,128)S(1)}, f32[80,4,2304]{2,1,0:T(4,128)S(1)}) fusion(f32[80,4,2304]{2,1,0:T(4,128)S(1)} %copy-done, f32[80,4,2304]{2,1,0:T(4,128)} %reshape.387), kind=kLoop, calls=%fused_computation.210 | loop fusion | flops 1465344 | bytes 8884224 | tf_op jit(solution)/shard_map/reduce_sum | solution.py:134
  249.6 2.2 convolution_add_fusion
  251.8 4.7 %reshape.393 = f32[80,4,2304]{2,1,0:T(4,128)} reshape(f32[80,9216]{1,0:T(8,128)} %convolution_add_fusion) | data formatting | bytes 5898240 | tf_op jit(solution)/shard_map/reshape | solution.py:150
  256.4 4.2 %add.227 = f32[80,4,2304]{2,1,0:T(4,128)} add(f32[80,4,2304]{2,1,0:T(4,128)S(1)} %copy-done.3, f32[80,4,2304]{2,1,0:T(4,128)} %reshape.393) | non-fusion elementwise | flops 737280 | bytes 8847360 | tf_op jit(solution)/shard_map/add | solution.py:150
  (131 shorter events, 26.4 us)
Async XLA Ops:
  9.8 7.1 %copy-start.19 = (s32[2,256]{1,0:T(2,128)S(1)}, s32[2,256]{1,0:T(2,128)}, u32[]{:S(2)}) copy-start(s32[2,256]{1,0:T(2,128)} %param.12) | copy-start | bytes 6148
  9.8 7.1 %copy-start.13 = (bf16[2,32,2304]{2,1,0:T(8,128)(2,1)S(1)}, bf16[2,32,2304]{2,1,0:T(8,128)(2,1)}, u32[]{:S(2)}) copy-start(bf16[2,32,2304]{2,1,0:T(8,128)(2,1)} %param.16) | copy-start | bytes 884740
  9.8 7.8 %copy-start = (f32[80,4,2304]{2,1,0:T(4,128)S(1)}, f32[80,4,2304]{2,1,0:T(4,128)}, u32[]{:S(2)}) copy-start(f32[80,4,2304]{2,1,0:T(4,128)} %param.11) | copy-start | bytes 8847364
  9.8 213.0 %all-to-all-start = ((bf16[8,2,32,2304]{3,2,1,0:T(8,128)(2,1)}), bf16[8,2,32,2304]{3,2,1,0:T(8,128)(2,1)}, u32[]{:S(2)}, u32[]{:S(2)}) async-start(bf16[8,2,32,2304]{3,2,1,0:T(8,128)(2,1)} %broadcast_in_dim.147), calls=%async_computation | async-start | bytes 4718592 | tf_op jit(solution)/shard_map/all_to_all | solution.py:15
  16.8 196.5 %all-reduce.3.cloned.1.call-start = ((), (), s32[]{:S(2)}) async-start(), calls=%async_computation.1 | async-start | bytes 2621440 | tf_op jit(solution)/shard_map/psum | solution.py:115
  21.1 15.1 %copy-start.17 = (f32[2,256,4]{1,2,0:T(4,128)S(1)}, f32[2,256,4]{1,2,0:T(4,128)}, u32[]{:S(2)}) copy-start(f32[2,256,4]{1,2,0:T(4,128)} %param.17) | copy-start | bytes 24580
  49.6 8.5 %copy-start.14 = (f32[256,80]{1,0:T(8,128)S(1)}, f32[256,80]{1,0:T(8,128)}, u32[]{:S(2)}) copy-start(f32[256,80]{1,0:T(8,128)} %gather_fusion.5) | copy-start | bytes 245764
  49.6 10.0 %copy-start.25 = (pred[256]{0:T(512)(128)(4,1)S(1)}, pred[256]{0:T(512)(128)(4,1)}, u32[]{:S(2)}) copy-start(pred[256]{0:T(512)(128)(4,1)} %get-tuple-element.29) | copy-start | bytes 772
  49.6 10.1 %copy-start.24 = (pred[256]{0:T(512)(128)(4,1)S(1)}, pred[256]{0:T(512)(128)(4,1)}, u32[]{:S(2)}) copy-start(pred[256]{0:T(512)(128)(4,1)} %get-tuple-element.24) | copy-start | bytes 772
  54.6 5.8 %copy-start.18 = (f32[2,256,4]{1,2,0:T(4,128)S(1)}, f32[2,256,4]{1,2,0:T(4,128)}, u32[]{:S(2)}) copy-start(f32[2,256,4]{1,2,0:T(4,128)} %param.17) | copy-start | bytes 24580
  54.7 6.4 %copy-start.26 = (f32[2,256]{1,0:T(2,128)S(1)}, f32[2,256]{1,0:T(2,128)}, u32[]{:S(2)}) copy-start(f32[2,256]{1,0:T(2,128)} %param.15) | copy-start | bytes 6148
  54.7 6.5 %copy-start.27 = (f32[2,256]{1,0:T(2,128)S(1)}, f32[2,256]{1,0:T(2,128)}, u32[]{:S(2)}) copy-start(f32[2,256]{1,0:T(2,128)} %param.14) | copy-start | bytes 6148
  54.7 6.5 %copy-start.28 = (f32[2,256]{1,0:T(2,128)S(1)}, f32[2,256]{1,0:T(2,128)}, u32[]{:S(2)}) copy-start(f32[2,256]{1,0:T(2,128)} %param.13) | copy-start | bytes 6148
  59.6 0.7 copy-start.12
  59.7 0.7 copy-start.11
  213.3 6.1 %copy-start.10 = (f32[256,256]{1,0:T(8,128)S(1)}, f32[256,256]{1,0:T(8,128)}, u32[]{:S(2)}) copy-start(f32[256,256]{1,0:T(8,128)} %get-tuple-element.16) | copy-start | bytes 786436
  217.0 5.7 %copy-start.6 = (bf16[256,80]{1,0:T(8,128)(2,1)}, bf16[256,80]{1,0:T(8,128)(2,1)S(1)}, u32[]{:S(2)}) copy-start(bf16[256,80]{1,0:T(8,128)(2,1)S(1)} %get-tuple-element.53) | copy-start | bytes 122884
  217.1 5.7 %copy-start.8 = (bf16[256,80]{1,0:T(8,128)(2,1)}, bf16[256,80]{1,0:T(8,128)(2,1)S(1)}, u32[]{:S(2)}) copy-start(bf16[256,80]{1,0:T(8,128)(2,1)S(1)} %get-tuple-element.54) | copy-start | bytes 122884
  225.4 1.4 copy-start.1
  225.4 1.4 copy-start.9
  225.4 1.4 copy-start.23
  227.3 0.8 copy-start.7
  228.2 0.7 copy-start.22
  229.5 0.7 copy-start.21
  230.7 0.7 copy-start.20
  239.9 2.9 %copy-start.4 = (bf16[1,2,32,2304]{3,2,0,1:T(8,128)(2,1)S(1)}, bf16[1,2,32,2304]{3,2,0,1:T(8,128)(2,1)}, u32[]{:S(2)}) copy-start(bf16[1,2,32,2304]{3,2,0,1:T(8,128)(2,1)} %get-tuple-element.45) | copy-start | bytes 884740
  239.9 2.9 %copy-start.5 = (bf16[1,2,32,2304]{3,2,0,1:T(8,128)(2,1)S(1)}, bf16[1,2,32,2304]{3,2,0,1:T(8,128)(2,1)}, u32[]{:S(2)}) copy-start(bf16[1,2,32,2304]{3,2,0,1:T(8,128)(2,1)} %get-tuple-element.46) | copy-start | bytes 884740
  242.7 1.6 copy-start.2
  242.9 1.4 copy-start.16
  247.0 0.8 copy-start.15
  251.7 4.7 %copy-start.3 = (f32[80,4,2304]{2,1,0:T(4,128)S(1)}, f32[80,4,2304]{2,1,0:T(4,128)}, u32[]{:S(2)}) copy-start(f32[80,4,2304]{2,1,0:T(4,128)} %copy-done.2) | copy-start | bytes 8847364
Sparse Core Ops, SparseCore 0:
  60.5 152.7 all-reduce.2
where the time goes:
time: 269 us; the launch traced here: 267 us
  waiting for transfers between devices  150 us (56%)
  local copies, waits for them, and re-layouts  48.4 us (18%)
  other arithmetic  31.1 us (12%)
  matrix products  16.3 us (6%)
  between operations  14.6 us (5%)
  starting transfers between devices  7.07 us (3%)
    psum x1, waiting for transfers between devices, on_device(): summed = lax.psum(tuple(pieces), ('slab', 'lev'))  150 us
    gather x4, local copies, waits for them, and re-layouts, cell_values(): picked = jnp.take(flattened, row_safe * slab_cols + col_safe, axis=1)  14.8 us
    unnamed x60, local copies, waits for them, and re-layouts  10.4 us
    reshape x2, local copies, waits for them, and re-layouts, on_device(): current = current + increment.reshape(members, lev_rows, slab_cols)  9.15 us
    dot_general x8, matrix products, regress_rows(): jnp.dot(gain_rows.T, mixed_rows, preferred_element_type=jnp.float32)  7.74 us
    all_to_all x1, starting transfers between devices, sent_to_all(): return lax.all_to_all(copies, axis, split_axis=0, concat_axis=0, tiled=True)  7.07 us
    transpose x4, other arithmetic, cell_values(): return jnp.where(inside[None, :], picked, 0.0).T  6.56 us
  transfers between devices with their start and end apart: 2, of which 1 were waited for; matrix products, arithmetic and copies ran while one was open for 21% of the time, Pallas kernels for 0%

commit v1 on v0

--- a/solution.py
+++ b/solution.py
@@ -112,7 +112,7 @@
             pieces.append(column_table(loc_column[earlier], columns))
             pieces.append(column_table(loc_column[earlier], next_cols))
             pieces.append(level_table(loc_level[earlier], levels))
-    summed = lax.psum(tuple(pieces), ("slab", "lev"))
+    summed = lax.psum(lax.psum(tuple(pieces), "slab"), "lev")
     raw_first = []
     raw_second = []
     position = 0

time: 269 us -> 272 us (1.011)
  waiting for transfers between devices: 150 us -> 153 us
    psum x1 -> x2, waiting for transfers between devices: 150 us -> 153 us  [on_device(): summed = lax.psum(lax.psum(tuple(pieces), 'slab'), 'lev')]
  transfers between devices with their start and end apart: 2 -> 3, of which waited for: 1 -> 2; matrix products, arithmetic and copies ran while one was open for 21% -> 20% of each run, Pallas kernels for 0% -> 0%
where the time goes in v1:
time: 272 us; the launch traced here: 270 us
  waiting for transfers between devices  153 us (56%)
  local copies, waits for them, and re-layouts  48.5 us (18%)
  other arithmetic  31 us (11%)
  matrix products  16.3 us (6%)
  between operations  14.6 us (5%)
  starting transfers between devices  7.11 us (3%)
    psum x2, waiting for transfers between devices, on_device(): summed = lax.psum(lax.psum(tuple(pieces), 'slab'), 'lev')  153 us
    gather x4, local copies, waits for them, and re-layouts, cell_values(): picked = jnp.take(flattened, row_safe * slab_cols + col_safe, axis=1)  14.8 us
    unnamed x60, local copies, waits for them, and re-layouts  10.6 us
    reshape x2, local copies, waits for them, and re-layouts, on_device(): current = current + increment.reshape(members, lev_rows, slab_cols)  9.17 us
    dot_general x8, matrix products, regress_rows(): jnp.dot(gain_rows.T, mixed_rows, preferred_element_type=jnp.float32)  7.77 us
    all_to_all x1, starting transfers between devices, sent_to_all(): return lax.all_to_all(copies, axis, split_axis=0, concat_axis=0, tiled=True)  7.07 us
    transpose x4, other arithmetic, cell_values(): return jnp.where(inside[None, :], picked, 0.0).T  6.57 us
  transfers between devices with their start and end apart: 3, of which 2 were waited for; matrix products, arithmetic and copies ran while one was open for 20% of the time, Pallas kernels for 0%

profile of v1, /device:TPU:1, one launch (start us, length us, event | category | flops | bytes accessed | tf_op | source)
XLA Modules:
  0.0 270.2 jit_solution(5789260087251405276)
XLA Ops:
  7.2 2.6 broadcast_in_dim.147
  9.8 7.1 %all-to-all-start = ((bf16[8,2,32,2304]{3,2,1,0:T(8,128)(2,1)}), bf16[8,2,32,2304]{3,2,1,0:T(8,128)(2,1)}, u32[]{:S(2)}, u32[]{:S(2)}) async-start(bf16[8,2,32,2304]{3,2,1,0:T(8,128)(2,1)} %broadcast_in_dim.147), calls=%async_computation | async-start | bytes 4718592 | tf_op jit(solution)/shard_map/all_to_all | solution.py:15
  17.6 3.6 %copy.35 = f32[80,4,2304]{0,2,1:T(8,128)} copy(f32[80,4,2304]{2,1,0:T(4,128)S(1)} %copy-done) | data formatting | bytes 5898240 | tf_op args[0]
  21.7 1.1 and_reduce_fusion.6
  23.4 3.7 %gather_fusion.2 = f32[256,80]{1,0:T(8,128)} fusion(f32[80,9216]{0,1:T(8,128)} %bitcast.212, s32[1024]{0:T(1024)S(1)} %pad_clamp_fusion.5), kind=kCustom, calls=%fused_computation.2.clone | custom fusion | bytes 164864 | tf_op jit(solution)/shard_map/jit(_take)/gather | solution.py:43
  27.1 3.7 %gather_fusion.1 = f32[256,80]{1,0:T(8,128)} fusion(f32[80,9216]{0,1:T(8,128)} %bitcast.213, s32[1024]{0:T(1024)S(1)} %pad_clamp_fusion.6), kind=kCustom, calls=%fused_computation.clone | custom fusion | bytes 164864 | tf_op jit(solution)/shard_map/jit(_take)/gather | solution.py:43
  32.5 3.7 %gather_fusion.3 = f32[256,80]{1,0:T(8,128)} fusion(f32[80,9216]{0,1:T(8,128)} %bitcast.214, s32[1024]{0:T(1024)S(1)} %pad_clamp_fusion.4), kind=kCustom, calls=%fused_computation.3.clone | custom fusion | bytes 164864 | tf_op jit(solution)/shard_map/jit(_take)/gather | solution.py:43
  38.0 1.2 copy.61
  39.2 1.5 gather_fusion.4
  41.6 1.2 pad_clamp_fusion.1
  42.8 3.8 %gather_fusion.5 = f32[256,80]{1,0:T(8,128)} fusion(f32[80,9216]{0,1:T(8,128)} %bitcast.215, s32[1024]{0:T(1024)} %pad_clamp_fusion.1), kind=kCustom, calls=%fused_computation.4.clone | custom fusion | bytes 164864 | tf_op jit(solution)/shard_map/jit(_take)/gather | solution.py:43
  46.6 1.2 pad_clamp_fusion
  47.8 1.6 gather_fusion.6
  50.4 1.7 fusion.45
  52.1 1.7 fusion.46
  54.5 1.7 fusion.44
  56.2 1.7 select_bitcast_fusion
  57.9 1.5 fusion.43
  61.7 87.5 %all-reduce.5.cloned.1.call-done = (f32[256,80]{1,0:T(8,128)}, f32[256,80]{1,0:T(8,128)}, f32[256,80]{1,0:T(8,128)}, f32[256,256]{1,0:T(8,128)}, f32[256,256]{1,...) async-done(((f32[256,80]{1,0:T(8,128)}, f32[256,80]{1,0:T(8,128)}, f32[256,80]{1,0:T(8,128)}, f32[256,256]{1,0:T(8,128)}, f32[256,256]{1,0:T(8,128)}, ...) | async-done | bytes 1114128 | tf_op jit(solution)/shard_map/psum | solution.py:115
  149.3 1.6 subtract_convert_fusion.1
  150.9 65.1 %all-reduce.7.cloned.1.call-done = (f32[256,80]{1,0:T(8,128)}, f32[256,80]{1,0:T(8,128)}, f32[256,80]{1,0:T(8,128)}, f32[256,256]{1,0:T(8,128)}, f32[256,256]{1,...) async-done(((f32[256,80]{1,0:T(8,128)}, f32[256,80]{1,0:T(8,128)}, f32[256,80]{1,0:T(8,128)}, f32[256,256]{1,0:T(8,128)}, f32[256,256]{1,0:T(8,128)}, ...) | async-done | bytes 1114128 | tf_op jit(solution)/shard_map/psum | solution.py:115
  217.1 1.2 fusion.80
  219.8 2.3 fusion.32
  222.1 1.7 fusion.87
  225.5 2.6 fusion.83
  228.2 1.2 copy-done.1
  235.9 2.2 convolution_add_fusion.3
  238.1 4.5 %reshape.387 = f32[80,4,2304]{2,1,0:T(4,128)} reshape(f32[80,9216]{1,0:T(8,128)} %convolution_add_fusion.3) | data formatting | bytes 5898240 | tf_op jit(solution)/shard_map/reshape | solution.py:150
  242.6 2.8 %fusion.79 = (f32[4,2304]{1,0:T(4,128)S(1)}, f32[80,4,2304]{2,1,0:T(4,128)S(1)}) fusion(f32[80,4,2304]{2,1,0:T(4,128)S(1)} %copy-done, f32[80,4,2304]{2,1,0:T(4,128)} %reshape.387), kind=kLoop, calls=%fused_computation.210 | loop fusion | flops 1465344 | bytes 8884224 | tf_op jit(solution)/shard_map/reduce_sum | solution.py:134
  252.3 2.2 convolution_add_fusion
  254.5 4.7 %reshape.393 = f32[80,4,2304]{2,1,0:T(4,128)} reshape(f32[80,9216]{1,0:T(8,128)} %convolution_add_fusion) | data formatting | bytes 5898240 | tf_op jit(solution)/shard_map/reshape | solution.py:150
  259.1 4.2 %add.241 = f32[80,4,2304]{2,1,0:T(4,128)} add(f32[80,4,2304]{2,1,0:T(4,128)S(1)} %copy-done.3, f32[80,4,2304]{2,1,0:T(4,128)} %reshape.393) | non-fusion elementwise | flops 737280 | bytes 8847360 | tf_op jit(solution)/shard_map/add | solution.py:150
  (134 shorter events, 27.5 us)
Async XLA Ops:
  9.8 7.1 %copy-start.19 = (s32[2,256]{1,0:T(2,128)S(1)}, s32[2,256]{1,0:T(2,128)}, u32[]{:S(2)}) copy-start(s32[2,256]{1,0:T(2,128)} %param.12) | copy-start | bytes 6148
  9.8 7.1 %copy-start.13 = (bf16[2,32,2304]{2,1,0:T(8,128)(2,1)S(1)}, bf16[2,32,2304]{2,1,0:T(8,128)(2,1)}, u32[]{:S(2)}) copy-start(bf16[2,32,2304]{2,1,0:T(8,128)(2,1)} %param.16) | copy-start | bytes 884740
  9.8 7.8 %copy-start = (f32[80,4,2304]{2,1,0:T(4,128)S(1)}, f32[80,4,2304]{2,1,0:T(4,128)}, u32[]{:S(2)}) copy-start(f32[80,4,2304]{2,1,0:T(4,128)} %param.11) | copy-start | bytes 8847364
  9.8 215.7 %all-to-all-start = ((bf16[8,2,32,2304]{3,2,1,0:T(8,128)(2,1)}), bf16[8,2,32,2304]{3,2,1,0:T(8,128)(2,1)}, u32[]{:S(2)}, u32[]{:S(2)}) async-start(bf16[8,2,32,2304]{3,2,1,0:T(8,128)(2,1)} %broadcast_in_dim.147), calls=%async_computation | async-start | bytes 4718592 | tf_op jit(solution)/shard_map/all_to_all | solution.py:15
  16.8 132.4 %all-reduce.5.cloned.1.call-start = ((), (), s32[]{:S(2)}) async-start(), calls=%async_computation.1 | async-start | bytes 2621440 | tf_op jit(solution)/shard_map/psum | solution.py:115
  21.1 15.0 %copy-start.17 = (f32[2,256,4]{1,2,0:T(4,128)S(1)}, f32[2,256,4]{1,2,0:T(4,128)}, u32[]{:S(2)}) copy-start(f32[2,256,4]{1,2,0:T(4,128)} %param.17) | copy-start | bytes 24580
  49.4 8.5 %copy-start.14 = (f32[256,80]{1,0:T(8,128)S(1)}, f32[256,80]{1,0:T(8,128)}, u32[]{:S(2)}) copy-start(f32[256,80]{1,0:T(8,128)} %gather_fusion.5) | copy-start | bytes 245764
  49.4 10.0 %copy-start.25 = (pred[256]{0:T(512)(128)(4,1)S(1)}, pred[256]{0:T(512)(128)(4,1)}, u32[]{:S(2)}) copy-start(pred[256]{0:T(512)(128)(4,1)} %get-tuple-element.36) | copy-start | bytes 772
  49.4 10.0 %copy-start.24 = (pred[256]{0:T(512)(128)(4,1)S(1)}, pred[256]{0:T(512)(128)(4,1)}, u32[]{:S(2)}) copy-start(pred[256]{0:T(512)(128)(4,1)} %get-tuple-element.31) | copy-start | bytes 772
  54.5 5.8 %copy-start.26 = (f32[2,256]{1,0:T(2,128)S(1)}, f32[2,256]{1,0:T(2,128)}, u32[]{:S(2)}) copy-start(f32[2,256]{1,0:T(2,128)} %param.15) | copy-start | bytes 6148
  54.5 5.8 %copy-start.27 = (f32[2,256]{1,0:T(2,128)S(1)}, f32[2,256]{1,0:T(2,128)}, u32[]{:S(2)}) copy-start(f32[2,256]{1,0:T(2,128)} %param.14) | copy-start | bytes 6148
  54.5 5.8 %copy-start.28 = (f32[2,256]{1,0:T(2,128)S(1)}, f32[2,256]{1,0:T(2,128)}, u32[]{:S(2)}) copy-start(f32[2,256]{1,0:T(2,128)} %param.13) | copy-start | bytes 6148
  59.4 0.7 copy-start.12
  59.5 0.7 copy-start.11
  60.3 155.8 %all-reduce.7.cloned.1.call-start = ((), (), s32[]{:S(2)}) async-start(), calls=%async_computation.2 | async-start | bytes 2621440 | tf_op jit(solution)/shard_map/psum | solution.py:115
  60.4 0.7 copy-start.18
  216.1 6.1 %copy-start.10 = (f32[256,256]{1,0:T(8,128)S(1)}, f32[256,256]{1,0:T(8,128)}, u32[]{:S(2)}) copy-start(f32[256,256]{1,0:T(8,128)} %get-tuple-element.23) | copy-start | bytes 786436
  219.8 5.7 %copy-start.6 = (bf16[256,80]{1,0:T(8,128)(2,1)}, bf16[256,80]{1,0:T(8,128)(2,1)S(1)}, u32[]{:S(2)}) copy-start(bf16[256,80]{1,0:T(8,128)(2,1)S(1)} %get-tuple-element.60) | copy-start | bytes 122884
  219.8 5.7 %copy-start.8 = (bf16[256,80]{1,0:T(8,128)(2,1)}, bf16[256,80]{1,0:T(8,128)(2,1)S(1)}, u32[]{:S(2)}) copy-start(bf16[256,80]{1,0:T(8,128)(2,1)S(1)} %get-tuple-element.61) | copy-start | bytes 122884
  228.1 1.4 copy-start.1
  228.1 1.4 copy-start.9
  228.1 1.4 copy-start.23
  230.0 0.8 copy-start.7
  230.9 0.7 copy-start.22
  232.2 0.7 copy-start.21
  233.4 0.7 copy-start.20
  242.6 2.9 %copy-start.4 = (bf16[1,2,32,2304]{3,2,0,1:T(8,128)(2,1)S(1)}, bf16[1,2,32,2304]{3,2,0,1:T(8,128)(2,1)}, u32[]{:S(2)}) copy-start(bf16[1,2,32,2304]{3,2,0,1:T(8,128)(2,1)} %get-tuple-element.52) | copy-start | bytes 884740
  242.6 2.9 %copy-start.5 = (bf16[1,2,32,2304]{3,2,0,1:T(8,128)(2,1)S(1)}, bf16[1,2,32,2304]{3,2,0,1:T(8,128)(2,1)}, u32[]{:S(2)}) copy-start(bf16[1,2,32,2304]{3,2,0,1:T(8,128)(2,1)} %get-tuple-element.53) | copy-start | bytes 884740
  245.4 1.6 copy-start.2
  245.6 1.4 copy-start.16
  249.7 0.8 copy-start.15
  254.5 4.7 %copy-start.3 = (f32[80,4,2304]{2,1,0:T(4,128)S(1)}, f32[80,4,2304]{2,1,0:T(4,128)}, u32[]{:S(2)}) copy-start(f32[80,4,2304]{2,1,0:T(4,128)} %copy-done.2) | copy-start | bytes 8847364
Sparse Core Ops, SparseCore 0:
  60.4 88.8 all-reduce.4
  152.2 63.8 all-reduce.6
